TPU v7x, 32 devices: a whole 2x2x4 slice. The times are simulated.
32 devices in a mesh: dp: 4 (over x, core), expert: 8 (over z, y).
Axes of the slice: x: 2, y: 2, z: 4, core: 2. Of those that a mesh axis runs over, the one named last changes fastest.
Arguments:
- tokens: bfloat16 [128, 256, 1280], P(('dp', 'expert')), may hold values from -32 to 32
- slot_keys: bfloat16 [1280, 8], replicated, may hold values from -20 to 20
- logit_scale: float32 [1], replicated, may hold values from 8 to 16
- up_weight: bfloat16 [8, 1280, 5120], P('expert', None, 'dp'), may hold values from -0.15625 to 0.15625
- up_bias: bfloat16 [8, 5120], P('expert', 'dp'), may hold values from -3 to 3
- down_weight: bfloat16 [8, 5120, 1280], P('expert', 'dp'), may hold values from -0.078125 to 0.078125
- down_bias: bfloat16 [8, 1280], replicated, may hold values from -3 to 3
Outputs:
- mixed_out: bfloat16 [128, 256, 1280], P(('dp', 'expert'))
All inputs are finite; a program needn't handle non-finite values.
Results may differ from a plain program's by a relative error of at most 0.017.
Values may be sent and summed in bfloat16 or wider, within the bound.
A program may use at most 64 MiB of HBM per device.

v0:
```python
import jax
import jax.numpy as jnp
from jax import lax
from jax.sharding import PartitionSpec as P

norm_eps = 1e-06


def unit_rms(values, axis_pos):
    return values * lax.rsqrt(jnp.mean(values * values, axis=axis_pos, keepdims=True) + norm_eps)


def body(tokens, slot_keys, logit_scale, up_weight, up_bias, down_weight, down_bias):
    images = tokens.shape[0]
    patches = tokens.shape[1]
    width = tokens.shape[2]
    per_owner = up_weight.shape[0]
    owners = lax.axis_size("expert")
    normed_tok = unit_rms(tokens.astype(jnp.float32), 2).astype(jnp.bfloat16)
    normed_keys = unit_rms(slot_keys.astype(jnp.float32), 0).astype(jnp.bfloat16)
    raw_scores = jnp.einsum(
        "ipd,dn->inp", normed_tok, normed_keys, preferred_element_type=jnp.float32
    )
    logits = logit_scale[0] * raw_scores / width
    dispatch = jax.nn.softmax(logits, axis=2).astype(jnp.bfloat16)
    combine = jax.nn.softmax(logits, axis=1).astype(jnp.bfloat16)
    slot_inputs = jnp.einsum(
        "inp,ipd->ind", dispatch, tokens, preferred_element_type=jnp.float32
    ).astype(jnp.bfloat16)
    routed = lax.all_to_all(slot_inputs, "expert", split_axis=1, concat_axis=0, tiled=True)
    pre = jnp.einsum(
        "rkd,kdf->rkf",
        lax.all_gather(routed, "dp", axis=0, tiled=True),
        up_weight,
        preferred_element_type=jnp.float32,
    )
    pre = pre + up_bias.astype(jnp.float32)[None]
    hidden = jax.nn.gelu(pre, approximate=False).astype(jnp.bfloat16)
    summed = lax.psum_scatter(
        jnp.einsum("rkf,kfd->rkd", hidden, down_weight, preferred_element_type=jnp.float32).astype(
            jnp.bfloat16
        ),
        "dp",
        scatter_dimension=0,
        tiled=True,
    ).astype(jnp.float32)
    own_bias = lax.dynamic_slice_in_dim(
        down_bias, lax.axis_index("expert") * per_owner, per_owner, 0
    ).astype(jnp.float32)
    finished = (
        (summed + own_bias[None]).astype(jnp.bfloat16).reshape(owners, images, per_owner, width)
    )
    returned = lax.all_to_all(finished, "expert", split_axis=0, concat_axis=0, tiled=True)
    weights = combine.reshape(images, owners, per_owner, patches)
    mixed_out = jnp.einsum("iekp,eikd->ipd", weights, returned, preferred_element_type=jnp.float32)
    return mixed_out.astype(jnp.bfloat16)


def solution(mesh):
    return jax.shard_map(
        body,
        mesh=mesh,
        in_specs=(
            P(("dp", "expert"), None, None),
            P(),
            P(),
            P("expert", None, "dp"),
            P("expert", "dp"),
            P("expert", "dp", None),
            P(),
        ),
        out_specs=P(("dp", "expert"), None, None),
        check_vma=False,
    )
```

profile of v0, /device:TPU:0, one launch (start us, length us, event | category | flops | bytes accessed | tf_op | source)
XLA Modules:
  0.0 83.9 jit_solution(10107239753829949492)
XLA Ops:
  6.5 0.0 copy-start
  7.3 1.0 %fusion.96 = f32[8]{0:T(128)S(1)} fusion(bf16[1280,8]{0,1:T(8,128)(2,1)} %param.8), kind=kLoop, calls=%fused_computation.87 | loop fusion | flops 30712 | bytes 20512 | tf_op jit(solution)/shard_map/reduce_sum | solution.py:10
  8.4 2.3 %fusion.2 = f32[4,256]{1,0:T(4,128)S(1)} fusion(bf16[4,256,1280]{2,1,0:T(8,128)(2,1)} %param.7), kind=kLoop, calls=%fused_computation.4 | loop fusion | flops 3931136 | bytes 2625536 | tf_op jit(solution)/shard_map/reduce_sum | solution.py:10
  10.7 0.0 copy-start.1
  10.7 2.6 %fusion.33 = f32[4,8,256]{2,1,0:T(8,128)S(1)} fusion(bf16[4,256,1280]{2,1,0:T(8,128)(2,1)} %param.7, f32[4,256]{1,0:T(4,128)S(1)} %add_rsqrt_fusion, bf16[1280,8]{0,1:T(8,128)(2,1)} %param.8, f32[8]{0:T(128)S(1)} %add_rsqrt_fusion.1, f32[]{:T(128)} %bitcast.139), kind=kOutput, calls=%fused_computation.24 | convolution fusion | flops 24950784 | bytes 2678820 | tf_op jit(solution)/shard_map/ipd,dn->inp/dot_general | solution.py:21
  13.3 0.2 fusion.133
  13.5 2.2 %convolution_convert_fusion.1 = bf16[4,8,1280]{2,1,0:T(8,128)(2,1)S(1)} fusion(bf16[4,256,1280]{2,1,0:T(8,128)(2,1)} %param.7, f32[4,8]{1,0:T(4,128)S(1)} %fusion.133, f32[4,8,256]{2,1,0:T(8,128)S(1)} %fusion.33), kind=kOutput, calls=%fused_computation.17 | convolution fusion | flops 21037344 | bytes 2736256 | tf_op jit(solution)/shard_map/inp,ipd->ind/dot_general | solution.py:27
  15.8 0.7 copy.11
  16.4 7.3 %all-to-all-start = ((bf16[4,8,1280]{2,0,1:T(4,128)(2,1)}), bf16[4,8,1280]{2,0,1:T(4,128)(2,1)S(1)}, u32[]{:S(2)}, u32[]{:S(2)}) async-start(bf16[4,8,1280]{2,0,1:T(4,128)(2,1)} %copy.11), calls=%async_computation | async-start | bytes 163840 | tf_op jit(solution)/shard_map/all_to_all | solution.py:30
  23.7 0.0 reduce-scatter.2.cloned.1.call-start
  23.8 0.0 copy-done.1
  23.8 6.9 %all-to-all-done = bf16[4,8,1280]{2,0,1:T(4,128)(2,1)S(1)} async-done(((bf16[4,8,1280]{2,0,1:T(4,128)(2,1)}), bf16[4,8,1280]{2,0,1:T(4,128)(2,1)S(1)}, u32[]{:S(2)}, u32[]{:S(2)}) %all-to-all-start) | async-done | bytes 81952 | tf_op jit(solution)/shard_map/all_to_all | solution.py:30
  30.8 6.6 %all_gather.3 = bf16[128,1,1280]{2,0,1:T(8,128)(2,1)} all-gather(bf16[32,1,1280]{2,0,1:T(8,128)(2,1)S(1)} %all_to_all.19), channel_id=1, replica_groups=mesh['dp'=4,'expert'=8] {'dp'}, dimensions={0}, use_global_device_ids=true | all-gather | bytes 409600 | tf_op jit(solution)/shard_map/all_gather | solution.py:33
  37.3 0.0 copy-done
  37.3 5.2 %fusion.20 = bf16[128,1,1280]{2,0,1:T(8,128)(2,1)} fusion(bf16[1,1280,1280]{2,1,0:T(8,128)(2,1)S(1)} %copy-done, bf16[1,1280,1280]{2,1,0:T(8,128)(2,1)} %param.10, bf16[128,1,1280]{2,0,1:T(8,128)(2,1)} %all_gather.3, f32[1280]{0:T(1024)S(1)} %convert_reduce_fusion.1), kind=kOutput, calls=%fused_computation.16 | convolution fusion | flops 849838080 | bytes 7214080 | tf_op jit(solution)/shard_map/rkf,kfd->rkd/dot_general | solution.py:40
  42.6 0.0 reduce-scatter.2.cloned.1.call-update
  42.6 0.8 convert_reduce_fusion
  43.3 17.3 %reduce-scatter.2.cloned.1.call-done = bf16[32,1,1280]{2,0,1:T(8,128)(2,1)} async-done(((bf16[128,1,1280]{2,0,1:T(8,128)(2,1)}), bf16[32,1,1280]{2,0,1:T(8,128)(2,1)}) %reduce-scatter.2.cloned.1.call-update) | async-done | bytes 81936 | tf_op jit(solution)/shard_map/reduce_scatter | solution.py:39
  60.6 0.9 %add_convert_fusion = bf16[32,1,1280]{2,0,1:T(8,128)(2,1)S(1)} fusion(bf16[32,1,1280]{2,0,1:T(8,128)(2,1)} %reduce-scatter.2.cloned.1.call-done, f32[1280]{0:T(1024)S(1)} %convert_reduce_fusion), kind=kLoop, calls=%fused_computation.82 | loop fusion | flops 122880 | bytes 168960 | tf_op jit(solution)/shard_map/convert_element_type | solution.py:51
  61.5 0.7 reshape.56
  62.2 5.5 %all-to-all-start.1 = ((bf16[8,4,1,1280]{3,1,2,0:T(4,128)(2,1)}), bf16[8,4,1,1280]{3,1,2,0:T(4,128)(2,1)S(1)}, u32[]{:S(2)}, u32[]{:S(2)}) async-start(bf16[8,4,1,1280]{3,1,2,0:T(4,128)(2,1)} %bitcast.16), calls=%async_computation.2 | async-start | bytes 163840 | tf_op jit(solution)/shard_map/all_to_all | solution.py:53
  67.7 7.0 %all-to-all-done.1 = bf16[8,4,1,1280]{3,1,2,0:T(4,128)(2,1)S(1)} async-done(((bf16[8,4,1,1280]{3,1,2,0:T(4,128)(2,1)}), bf16[8,4,1,1280]{3,1,2,0:T(4,128)(2,1)S(1)}, u32[]{:S(2)}, u32[]{:S(2)}) %all-to-all-start.1) | async-done | bytes 81952 | tf_op jit(solution)/shard_map/all_to_all | solution.py:53
  74.7 2.4 %convolution_convert_fusion = bf16[4,256,1280]{2,1,0:T(8,128)(2,1)} fusion(bf16[8,4,1,1280]{3,1,2,0:T(4,128)(2,1)S(1)} %all-to-all-done.1, f32[4,256]{1,0:T(4,128)S(1)} %fusion.134, f32[4,8,256]{2,1,0:T(8,128)S(1)} %fusion.33), kind=kOutput, calls=%fused_computation.6 | convolution fusion | flops 22307848 | bytes 2740224 | tf_op jit(solution)/shard_map/iekp,eikd->ipd/dot_general | solution.py:55
  (5 shorter events, 0.1 us)
Async XLA Ops:
  6.5 30.8 %copy-start = (bf16[1,1280,1280]{2,1,0:T(8,128)(2,1)S(1)}, bf16[1,1280,1280]{2,1,0:T(8,128)(2,1)}, u32[]{:S(2)}) copy-start(bf16[1,1280,1280]{2,1,0:T(8,128)(2,1)} %param.12) | copy-start | bytes 9830404
  10.7 13.1 %copy-start.1 = (bf16[1,1280]{1,0:T(2,128)(2,1)S(1)}, bf16[1,1280]{1,0:T(2,128)(2,1)}, u32[]{:S(2)}) copy-start(bf16[1,1280]{1,0:T(2,128)(2,1)} %param.11) | copy-start | bytes 7684
  16.4 14.3 %all-to-all-start = ((bf16[4,8,1280]{2,0,1:T(4,128)(2,1)}), bf16[4,8,1280]{2,0,1:T(4,128)(2,1)S(1)}, u32[]{:S(2)}, u32[]{:S(2)}) async-start(bf16[4,8,1280]{2,0,1:T(4,128)(2,1)} %copy.11), calls=%async_computation | async-start | bytes 163840 | tf_op jit(solution)/shard_map/all_to_all | solution.py:30
  23.7 36.9 %reduce-scatter.2.cloned.1.call-start = ((), (), s32[]{:S(2)}) async-start(), calls=%async_computation.3 | async-start | bytes 409600 | tf_op jit(solution)/shard_map/reduce_scatter | solution.py:39
  62.2 12.5 %all-to-all-start.1 = ((bf16[8,4,1,1280]{3,1,2,0:T(4,128)(2,1)}), bf16[8,4,1,1280]{3,1,2,0:T(4,128)(2,1)S(1)}, u32[]{:S(2)}, u32[]{:S(2)}) async-start(bf16[8,4,1,1280]{3,1,2,0:T(4,128)(2,1)} %bitcast.16), calls=%async_computation.2 | async-start | bytes 163840 | tf_op jit(solution)/shard_map/all_to_all | solution.py:53
Sparse Core Ops, SparseCore 0:
  42.7 17.8 reduce-scatter.1
where the time goes:
time: 84.4 us; the launch traced here: 83.9 us
  waiting for transfers between devices  31.2 us (37%)
  between operations  14.2 us (17%)
  starting transfers between devices  12.8 us (15%)
  matrix products  12.5 us (15%)
  blocking collectives  6.55 us (8%)
  other arithmetic  5.26 us (6%)
  local copies, waits for them, and re-layouts  1.37 us (2%)
    reduce_scatter x1, waiting for transfers between devices, body(): lax.psum_scatter(jnp.einsum('rkf,kfd->rkd', hidden, down_weight, preferre...  17.3 us
    all_to_all x1, starting transfers between devices, body(): lax.all_to_all(slot_inputs, 'expert', split_axis=1, concat_axis=0, tiled=...  7.31 us
    all_to_all x1, waiting for transfers between devices, body(): lax.all_to_all(finished, 'expert', split_axis=0, concat_axis=0, tiled=True)  6.98 us
    all_to_all x1, waiting for transfers between devices, body(): lax.all_to_all(slot_inputs, 'expert', split_axis=1, concat_axis=0, tiled=...  6.93 us
    all_gather x1, blocking collectives, body(): lax.all_gather(routed, 'dp', axis=0, tiled=True)  6.55 us
    all_to_all x1, starting transfers between devices, body(): lax.all_to_all(finished, 'expert', split_axis=0, concat_axis=0, tiled=True)  5.5 us
    dot_general x1, matrix products, body(): jnp.einsum('rkf,kfd->rkd', hidden, down_weight, preferred_element_type=jn...  5.22 us
    reduce_sum x2, other arithmetic, unit_rms(): jnp.mean(values * values, axis=axis_pos, keepdims=True) + norm_eps  3.35 us
  transfers between devices with their start and end apart: 3, of which 3 were waited for; matrix products, arithmetic and copies ran while one was open for 1% of the time, Pallas kernels for 0%

commit v1 on v0

v1 whole, which is shorter than its diff:
```python
import functools

import jax
import jax.numpy as jnp
from jax import lax
from jax.experimental import pallas as pl
from jax.experimental.pallas import tpu as pltpu
from jax.sharding import PartitionSpec as P

MESH = pl.DeviceIdType.MESH
F32 = jnp.float32
BF16 = jnp.bfloat16
norm_eps = 1e-06
NT = (((1,), (1,)), ((), ()))
CORES = 2


def erf_gelu(v):
    return 0.5 * v * (1.0 + lax.erf(v * 0.7071067811865476))


def route_and_experts(
    owners,
    n_dp,
    chunk,
    tok_hbm,
    keys_ref,
    scale_ref,
    w1_hbm,
    b1_ref,
    w2_hbm,
    b2_ref,
    comb_ref,
    ret_ref,
    tok,
    w1,
    w2,
    send,
    recv,
    xf,
    hid,
    part,
    mine,
    pair,
    back,
    got,
    tok_sem,
    w_sem,
    own_sem,
    s_send,
    s_recv,
    r_send,
    r_recv,
    p_send,
    p_recv,
    b_send,
    b_recv,
):
    images, patches, width = tok.shape
    hidden = w1.shape[1]
    halves = n_dp // CORES
    groups = halves * owners
    rows = groups * images
    slots = owners * images

    d = lax.axis_index("dp")
    e = lax.axis_index("expert")
    core = lax.rem(d, CORES)
    half = lax.div(d, CORES)
    me = half * owners + e
    other = 1 - core
    partner = {"dp": half * CORES + other, "expert": e}

    def device(t):
        return {"dp": lax.div(t, owners) * CORES + core, "expert": lax.rem(t, owners)}

    for i in range(images):
        pltpu.make_async_copy(tok_hbm.at[i], tok.at[i], tok_sem.at[i]).start()
    load1 = pltpu.make_async_copy(w1_hbm.at[0], w1, w_sem.at[0])
    load2 = pltpu.make_async_copy(w2_hbm.at[0], w2, w_sem.at[1])
    load1.start()
    load2.start()

    barrier = pltpu.get_barrier_semaphore()
    pl.semaphore_signal(barrier, inc=1, device_id=partner, device_id_type=MESH)

    def greet(k, c):
        t = lax.rem(me + k, groups)
        pl.semaphore_signal(barrier, inc=1, device_id=device(t), device_id_type=MESH)
        return c

    lax.fori_loop(1, groups, greet, 0)

    keys = keys_ref[...].astype(F32)
    keys = keys * lax.rsqrt(jnp.mean(keys * keys, axis=0, keepdims=True) + norm_eps)
    slot_of = lax.broadcasted_iota(jnp.int32, (slots, owners), 0) // images
    col = lax.broadcasted_iota(jnp.int32, (slots, owners), 1)
    spread = jnp.where(slot_of == col, 1.0, 0.0).astype(BF16)
    keys = lax.dot_general(spread, keys.astype(BF16), NT, preferred_element_type=F32)
    keys = keys.astype(BF16)
    ones = jnp.ones((16, width), BF16)
    factor = scale_ref[0] / width
    image_of = lax.broadcasted_iota(jnp.int32, (slots, patches), 0) % images

    total = None
    for i in range(images):
        pltpu.make_async_copy(tok_hbm.at[i], tok.at[i], tok_sem.at[i]).wait()
        t = tok[i]
        raw = lax.dot_general(keys, t, NT, preferred_element_type=F32)
        squares = lax.dot_general(ones, t * t, NT, preferred_element_type=F32)[0:1]
        logits = raw * (lax.rsqrt(squares / width + norm_eps) * factor)
        keep = image_of == i
        up = jnp.exp(logits - jnp.max(logits, axis=1, keepdims=True))
        up = up / jnp.sum(up, axis=1, keepdims=True)
        dispatch = jnp.where(keep, up, 0.0).astype(BF16)
        term = jnp.dot(dispatch, t, preferred_element_type=F32)
        total = term if total is None else total + term
        mix = jnp.exp(logits - jnp.max(logits, axis=0, keepdims=True))
        mix = mix * (images / jnp.sum(mix, axis=0, keepdims=True))
        comb_ref[i] = jnp.where(keep, mix, 0.0).astype(BF16)
    for n in range(owners):
        send[n] = total[n * images : (n + 1) * images].astype(BF16)

    pl.semaphore_wait(barrier, groups)

    def out_copy(t):
        return pltpu.make_async_remote_copy(
            src_ref=send.at[lax.rem(t, owners)],
            dst_ref=recv.at[core, me],
            send_sem=s_send.at[t],
            recv_sem=s_recv.at[me],
            device_id=device(t),
            device_id_type=MESH,
        )

    def in_copy(t):
        return pltpu.make_async_remote_copy(
            src_ref=send.at[0],
            dst_ref=recv.at[core, t],
            send_sem=s_send.at[t],
            recv_sem=s_recv.at[t],
            device_id=device(t),
            device_id_type=MESH,
        )

    def relay(side, t):
        return pltpu.make_async_remote_copy(
            src_ref=recv.at[side, t],
            dst_ref=recv.at[side, t],
            send_sem=r_send.at[t],
            recv_sem=r_recv.at[t],
            device_id=partner,
            device_id_type=MESH,
        )

    own = pltpu.make_async_copy(send.at[e], recv.at[core, me], own_sem.at[0])
    own.start()

    def start_out(k, c):
        out_copy(lax.rem(me + k, groups)).start()
        return c

    lax.fori_loop(1, groups, start_out, 0)
    own.wait()
    relay(core, me).start()

    def pass_on(k, c):
        t = lax.rem(me + groups - k, groups)
        in_copy(t).wait_recv()
        relay(core, t).start()
        return c

    lax.fori_loop(1, groups, pass_on, 0)

    def take(k, c):
        relay(other, k).wait_recv()
        return c

    lax.fori_loop(0, groups, take, 0)

    for side in range(CORES):

        def place(k, c):
            pairs = [recv[side, 2 * k + q].astype(F32) for q in range(2)]
            at = pl.multiple_of(side * rows + k * 2 * images, 2 * images)
            xf[pl.ds(at, 2 * images), :] = jnp.concatenate(pairs, axis=0)
            return c

        lax.fori_loop(0, groups // 2, place, 0, unroll=groups <= 16)

    load1.wait()
    block = min(128, CORES * rows)
    steps = CORES * rows // block

    def first(m, c):
        at = pl.multiple_of(m * block, block)
        x = xf[pl.ds(at, block), :].astype(BF16)
        for j in range(0, hidden, chunk):
            v = jnp.dot(x, w1[:, j : j + chunk], preferred_element_type=F32)
            v = v + b1_ref[0:1, j : j + chunk].astype(F32)
            hid[pl.ds(at, block), j : j + chunk] = erf_gelu(v).astype(BF16)
        return c

    lax.fori_loop(0, steps, first, 0, unroll=steps == 1)
    load2.wait()

    def pair_copy(j):
        return pltpu.make_async_remote_copy(
            src_ref=part.at[j, other],
            dst_ref=pair.at[j],
            send_sem=p_send.at[j],
            recv_sem=p_recv.at[j],
            device_id=partner,
            device_id_type=MESH,
        )

    pieces = width // chunk
    for j in range(pieces):
        for side in range(CORES):

            def second(m, c):
                at = pl.multiple_of(m * block2, block2)
                h = hid[pl.ds(side * rows + at, block2), :]
                v = jnp.dot(h, w2[:, j * chunk : (j + 1) * chunk], preferred_element_type=F32)
                part[j, side, pl.ds(at, block2), :] = v.astype(BF16)
                mine[j, side, pl.ds(at, block2), :] = v
                return c

            block2 = min(128, rows)
            lax.fori_loop(0, rows // block2, second, 0, unroll=rows == block2)
        pair_copy(j).start()

    for j in range(pieces):
        pair_copy(j).wait_recv()

        def join(k, c):
            at = pl.multiple_of(k * 4 * images, 4 * images)
            v = mine[j, core, pl.ds(at, 4 * images), :]
            v = v + pair[j, pl.ds(at, 4 * images), :].astype(F32)
            for q in range(4):
                back[4 * k + q, :, j * chunk : (j + 1) * chunk] = v[
                    q * images : (q + 1) * images
                ].astype(BF16)
            return c

        lax.fori_loop(0, groups // 4, join, 0, unroll=groups <= 16)

    def home(t):
        return pltpu.make_async_remote_copy(
            src_ref=back.at[t],
            dst_ref=got.at[me],
            send_sem=b_send.at[t],
            recv_sem=b_recv.at[me],
            device_id=device(t),
            device_id_type=MESH,
        )

    def landed(t):
        return pltpu.make_async_remote_copy(
            src_ref=back.at[t],
            dst_ref=got.at[t],
            send_sem=b_send.at[t],
            recv_sem=b_recv.at[t],
            device_id=device(t),
            device_id_type=MESH,
        )

    keep_own = pltpu.make_async_copy(back.at[me], got.at[me], own_sem.at[1])
    keep_own.start()

    def start_home(k, c):
        home(lax.rem(me + k, groups)).start()
        return c

    lax.fori_loop(1, groups, start_home, 0)

    def end_sends(k, c):
        out_copy(lax.rem(me + k, groups)).wait_send()
        return c

    lax.fori_loop(1, groups, end_sends, 0)

    def end_relays(k, c):
        relay(core, k).wait_send()
        return c

    lax.fori_loop(0, groups, end_relays, 0)
    for j in range(pieces):
        pair_copy(j).wait_send()
    keep_own.wait()

    def arrive(k, c):
        landed(lax.rem(me + groups - k, groups)).wait_recv()
        return c

    lax.fori_loop(1, groups, arrive, 0)
    bias = b2_ref[...].astype(F32)
    for n in range(0, owners, 2):
        both = []
        for q in (n, n + 1):
            v = got[q].astype(F32)
            for x in range(1, halves):
                v = v + got[x * owners + q].astype(F32)
            both.append(v + bias[q : q + 1])
        ret_ref[n * images : (n + 2) * images, :] = jnp.concatenate(both, axis=0)

    def end_home(k, c):
        home(lax.rem(me + k, groups)).wait_send()
        return c

    lax.fori_loop(1, groups, end_home, 0)


def mix_kernel(comb_ref, ret_ref, out_ref):
    out_ref[0] = lax.dot_general(
        comb_ref[0],
        ret_ref[...].astype(BF16),
        (((0,), (0,)), ((), ())),
        preferred_element_type=F32,
    ).astype(out_ref.dtype)


def body(tokens, slot_keys, logit_scale, up_weight, up_bias, down_weight, down_bias):
    images, patches, width = tokens.shape
    owners = lax.axis_size("expert")
    n_dp = lax.axis_size("dp")
    hidden = up_weight.shape[2]
    halves = n_dp // CORES
    groups = halves * owners
    rows = groups * images
    slots = owners * images
    chunk = 256
    pieces = width // chunk
    vmem = pl.BlockSpec(memory_space=pltpu.VMEM)
    hbm = pl.BlockSpec(memory_space=pl.ANY)
    dma = pltpu.SemaphoreType.DMA
    comb, ret = pl.pallas_call(
        functools.partial(route_and_experts, owners, n_dp, chunk),
        out_shape=(
            jax.ShapeDtypeStruct((images, slots, patches), BF16),
            jax.ShapeDtypeStruct((slots, width), F32),
        ),
        in_specs=[
            hbm,
            vmem,
            pl.BlockSpec(memory_space=pltpu.SMEM),
            hbm,
            vmem,
            hbm,
            vmem,
        ],
        out_specs=(vmem, vmem),
        scratch_shapes=[
            pltpu.VMEM((images, patches, width), BF16),
            pltpu.VMEM((width, hidden), BF16),
            pltpu.VMEM((hidden, width), BF16),
            pltpu.VMEM((owners, images, width), BF16),
            pltpu.VMEM((CORES, groups, images, width), BF16),
            pltpu.VMEM((CORES * rows, width), F32),
            pltpu.VMEM((CORES * rows, hidden), BF16),
            pltpu.VMEM((pieces, CORES, rows, chunk), BF16),
            pltpu.VMEM((pieces, CORES, rows, chunk), F32),
            pltpu.VMEM((pieces, rows, chunk), BF16),
            pltpu.VMEM((groups, images, width), BF16),
            pltpu.VMEM((groups, images, width), BF16),
            dma((images,)),
            dma((2,)),
            dma((2,)),
            dma((groups,)),
            dma((groups,)),
            dma((groups,)),
            dma((groups,)),
            dma((pieces,)),
            dma((pieces,)),
            dma((groups,)),
            dma((groups,)),
        ],
        compiler_params=pltpu.CompilerParams(
            collective_id=0, has_side_effects=True, vmem_limit_bytes=60 * 1024 * 1024
        ),
        name="route_and_experts",
    )(tokens, slot_keys, logit_scale, up_weight, up_bias, down_weight, down_bias)
    return pl.pallas_call(
        mix_kernel,
        grid=(images,),
        out_shape=jax.ShapeDtypeStruct(tokens.shape, BF16),
        in_specs=[
            pl.BlockSpec((1, slots, patches), lambda i: (i, 0, 0)),
            pl.BlockSpec((slots, width), lambda i: (0, 0)),
        ],
        out_specs=pl.BlockSpec((1, patches, width), lambda i: (i, 0, 0)),
        name="mix_tokens",
    )(comb, ret)


def solution(mesh):
    return jax.shard_map(
        body,
        mesh=mesh,
        in_specs=(
            P(("dp", "expert"), None, None),
            P(),
            P(),
            P("expert", None, "dp"),
            P("expert", "dp"),
            P("expert", "dp", None),
            P(),
        ),
        out_specs=P(("dp", "expert"), None, None),
        check_vma=False,
    )
```

time: 84.4 us -> 32.3 us (0.38)
  waiting for transfers between devices: 31.2 us -> 0 us
  Pallas kernels: 0 us -> 29.7 us
  between operations: 14.2 us -> 0.66 us
  starting transfers between devices: 12.8 us -> 0 us
  matrix products: 12.5 us -> 0 us
  blocking collectives: 6.55 us -> 0 us
  other arithmetic: 5.26 us -> 0 us
    pallas_call x0 -> x2, Pallas kernels: none -> 29.7 us  [the longest x1 25.7 us: body(): pl.pallas_call(functools.partial(route_and_experts, owners, n_dp, chunk),...]
    reduce_scatter x1 -> x0, waiting for transfers between devices: 17.3 us -> none  [body(): lax.psum_scatter(jnp.einsum('rkf,kfd->rkd', hidden, down_weight, preferre...]
    all_to_all x2 -> x0, waiting for transfers between devices: 13.9 us -> none  [the longest x1 6.98 us: body(): lax.all_to_all(finished, 'expert', split_axis=0, concat_axis=0, tiled=True)]
    all_to_all x2 -> x0, starting transfers between devices: 12.8 us -> none  [the longest x1 7.31 us: body(): lax.all_to_all(slot_inputs, 'expert', split_axis=1, concat_axis=0, tiled=...]
    dot_general x4 -> x0, matrix products: 12.5 us -> none  [the longest x1 5.22 us: body(): jnp.einsum('rkf,kfd->rkd', hidden, down_weight, preferred_element_type=jn...]
    all_gather x1 -> x0, blocking collectives: 6.55 us -> none  [body(): lax.all_gather(routed, 'dp', axis=0, tiled=True)]
    reduce_sum x2 -> x0, other arithmetic: 3.35 us -> none  [unit_rms(): jnp.mean(values * values, axis=axis_pos, keepdims=True) + norm_eps]
    unnamed x4 -> x1, local copies, waits for them, and re-layouts: 0.01 us -> 1.62 us
  transfers between devices with their start and end apart: 3 -> 0, of which waited for: 3 -> 0; matrix products, arithmetic and copies ran while one was open for 1% -> 0% of each run, Pallas kernels for 0% -> 0%
where the time goes in v1:
time: 32.3 us; the launch traced here: 32 us
  Pallas kernels  29.7 us (92%)
  local copies, waits for them, and re-layouts  1.62 us (5%)
  between operations  0.66 us (2%)
    pallas_call x1, Pallas kernels, body(): pl.pallas_call(functools.partial(route_and_experts, owners, n_dp, chunk),...  25.7 us
    pallas_call x1, Pallas kernels, body(): pl.pallas_call(mix_kernel, grid=(images,), out_shape=jax.ShapeDtypeStruct...  4.04 us
    unnamed x1, local copies, waits for them, and re-layouts  1.62 us

profile of v1, /device:TPU:0, one launch (start us, length us, event | category | flops | bytes accessed | tf_op | source)
XLA Modules:
  0.0 32.0 jit_solution(16095746842741412780)
XLA Ops:
  0.7 1.6 %copy.8.keys_ref = bf16[1280,8]{1,0:T(8,128)(2,1)} copy(bf16[1280,8]{0,1:T(8,128)(2,1)} %param.8) | data formatting | bytes 40960 | tf_op args[1]
  2.3 25.7 %route_and_experts.1 = (bf16[4,32,256]{2,1,0:T(8,128)(2,1)}, f32[32,1280]{1,0:T(8,128)}) custom-call(bf16[4,256,1280]{2,1,0:T(8,128)(2,1)} %tok_hbm.1, bf16[1280,8]{1,0:T(8,128)(2,1)} %copy.8.keys_ref, f32[1]{0:T(128)S(6)} %copy.9.scale_ref, bf16[1,1280,1280]{2,1,0:T(8,128)(2,1)} %w1_hbm.1, bf16[1,1280]{1,0:T(2,128)(2,1)} %b1_ref.1, ...), custom_call_target="tpu_custom_call" | custom-call | tf_op jit(solution)/shard_map/route_and_experts/pallas_call | solution.py:337
  28.0 4.0 %mix_tokens.1 = bf16[4,256,1280]{2,1,0:T(8,128)(2,1)} custom-call(bf16[4,32,256]{2,1,0:T(8,128)(2,1)} %get-tuple-element.7.comb_ref, f32[32,1280]{1,0:T(8,128)} %get-tuple-element.8.ret_ref), custom_call_target="tpu_custom_call" | custom-call | tf_op jit(solution)/shard_map/mix_tokens/pallas_call | solution.py:383

commit v2 on v1

--- a/solution.py
+++ b/solution.py
@@ -24,14 +24,18 @@
     n_dp,
     chunk,
     tok_hbm,
+    keys_hbm,
+    scale_hbm,
+    w1_hbm,
+    b1_hbm,
+    w2_hbm,
+    b2_hbm,
+    comb_ref,
+    ret_ref,
     keys_ref,
     scale_ref,
-    w1_hbm,
     b1_ref,
-    w2_hbm,
     b2_ref,
-    comb_ref,
-    ret_ref,
     tok,
     w1,
     w2,
@@ -44,6 +48,7 @@
     pair,
     back,
     got,
+    small_sem,
     tok_sem,
     w_sem,
     own_sem,
@@ -71,16 +76,41 @@
     other = 1 - core
     partner = {"dp": half * CORES + other, "expert": e}
 
+    quarter = max(1, owners // 4)
+    outward = [
+        (a, q * quarter + b)
+        for q in (2, 3, 1, 0)
+        for b in range(quarter)
+        for a in reversed(range(halves))
+        if q * quarter + b < owners and (a, q * quarter + b) != (0, 0)
+    ]
+    inward = outward[::-1]
+
+    def for_peers(act, order):
+        if groups <= 16:
+            for a, b in order:
+                act(lax.rem(half + a, halves) * owners + lax.rem(e + b, owners))
+        else:
+
+            def step(k, c):
+                act(lax.rem(me + k, groups))
+                return c
+
+            lax.fori_loop(1, groups, step, 0)
+
     def device(t):
         return {"dp": lax.div(t, owners) * CORES + core, "expert": lax.rem(t, owners)}
 
+    load_keys = pltpu.make_async_copy(keys_hbm, keys_ref, small_sem.at[0])
+    load_scale = pltpu.make_async_copy(scale_hbm, scale_ref, small_sem.at[1])
+    load_b1 = pltpu.make_async_copy(b1_hbm, b1_ref, small_sem.at[2])
+    load_b2 = pltpu.make_async_copy(b2_hbm, b2_ref, small_sem.at[3])
+    load_keys.start()
+    load_scale.start()
     for i in range(images):
         pltpu.make_async_copy(tok_hbm.at[i], tok.at[i], tok_sem.at[i]).start()
     load1 = pltpu.make_async_copy(w1_hbm.at[0], w1, w_sem.at[0])
     load2 = pltpu.make_async_copy(w2_hbm.at[0], w2, w_sem.at[1])
-    load1.start()
-    load2.start()
-
     barrier = pltpu.get_barrier_semaphore()
     pl.semaphore_signal(barrier, inc=1, device_id=partner, device_id_type=MESH)
 
@@ -91,33 +121,38 @@
 
     lax.fori_loop(1, groups, greet, 0)
 
+    load_keys.wait()
     keys = keys_ref[...].astype(F32)
-    keys = keys * lax.rsqrt(jnp.mean(keys * keys, axis=0, keepdims=True) + norm_eps)
+    keys = keys * lax.rsqrt(jnp.mean(keys * keys, axis=1, keepdims=True) + norm_eps)
     slot_of = lax.broadcasted_iota(jnp.int32, (slots, owners), 0) // images
     col = lax.broadcasted_iota(jnp.int32, (slots, owners), 1)
     spread = jnp.where(slot_of == col, 1.0, 0.0).astype(BF16)
-    keys = lax.dot_general(spread, keys.astype(BF16), NT, preferred_element_type=F32)
+    keys = jnp.dot(spread, keys.astype(BF16), preferred_element_type=F32)
     keys = keys.astype(BF16)
     ones = jnp.ones((16, width), BF16)
+    load_scale.wait()
     factor = scale_ref[0] / width
     image_of = lax.broadcasted_iota(jnp.int32, (slots, patches), 0) % images
 
-    total = None
+    scores = []
     for i in range(images):
         pltpu.make_async_copy(tok_hbm.at[i], tok.at[i], tok_sem.at[i]).wait()
         t = tok[i]
         raw = lax.dot_general(keys, t, NT, preferred_element_type=F32)
         squares = lax.dot_general(ones, t * t, NT, preferred_element_type=F32)[0:1]
-        logits = raw * (lax.rsqrt(squares / width + norm_eps) * factor)
-        keep = image_of == i
-        up = jnp.exp(logits - jnp.max(logits, axis=1, keepdims=True))
+        scores.append(raw * (lax.rsqrt(squares / width + norm_eps) * factor))
+    load1.start()
+    load2.start()
+    load_b1.start()
+    load_b2.start()
+    parts = []
+    for i in range(images):
+        up = jnp.exp(scores[i] - jnp.max(scores[i], axis=1, keepdims=True))
         up = up / jnp.sum(up, axis=1, keepdims=True)
-        dispatch = jnp.where(keep, up, 0.0).astype(BF16)
-        term = jnp.dot(dispatch, t, preferred_element_type=F32)
-        total = term if total is None else total + term
-        mix = jnp.exp(logits - jnp.max(logits, axis=0, keepdims=True))
-        mix = mix * (images / jnp.sum(mix, axis=0, keepdims=True))
-        comb_ref[i] = jnp.where(keep, mix, 0.0).astype(BF16)
+        parts.append(jnp.where(image_of == i, up, 0.0).astype(BF16))
+    total = jnp.zeros((slots, width), F32)
+    for i in range(images):
+        total = total + jnp.dot(parts[i], tok[i], preferred_element_type=F32)
     for n in range(owners):
         send[n] = total[n * images : (n + 1) * images].astype(BF16)
 
@@ -156,21 +191,22 @@
     own = pltpu.make_async_copy(send.at[e], recv.at[core, me], own_sem.at[0])
     own.start()
 
-    def start_out(k, c):
-        out_copy(lax.rem(me + k, groups)).start()
-        return c
-
-    lax.fori_loop(1, groups, start_out, 0)
+    def start_out(t):
+        out_copy(t).start()
+
+    for_peers(start_out, outward)
     own.wait()
     relay(core, me).start()
-
-    def pass_on(k, c):
-        t = lax.rem(me + groups - k, groups)
+    for i in range(images):
+        mix = jnp.exp(scores[i] - jnp.max(scores[i], axis=0, keepdims=True))
+        mix = mix * (images / jnp.sum(mix, axis=0, keepdims=True))
+        comb_ref[i] = jnp.where(image_of == i, mix, 0.0).astype(BF16)
+
+    def pass_on(t):
         in_copy(t).wait_recv()
         relay(core, t).start()
-        return c
-
-    lax.fori_loop(1, groups, pass_on, 0)
+
+    for_peers(pass_on, inward)
 
     def take(k, c):
         relay(other, k).wait_recv()
@@ -189,6 +225,8 @@
         lax.fori_loop(0, groups // 2, place, 0, unroll=groups <= 16)
 
     load1.wait()
+    load_b1.wait()
+    load_b2.wait()
     block = min(128, CORES * rows)
     steps = CORES * rows // block
 
@@ -268,11 +306,10 @@
     keep_own = pltpu.make_async_copy(back.at[me], got.at[me], own_sem.at[1])
     keep_own.start()
 
-    def start_home(k, c):
-        home(lax.rem(me + k, groups)).start()
-        return c
-
-    lax.fori_loop(1, groups, start_home, 0)
+    def start_home(t):
+        home(t).start()
+
+    for_peers(start_home, outward)
 
     def end_sends(k, c):
         out_copy(lax.rem(me + k, groups)).wait_send()
@@ -311,13 +348,19 @@
     lax.fori_loop(1, groups, end_home, 0)
 
 
-def mix_kernel(comb_ref, ret_ref, out_ref):
-    out_ref[0] = lax.dot_general(
-        comb_ref[0],
-        ret_ref[...].astype(BF16),
-        (((0,), (0,)), ((), ())),
-        preferred_element_type=F32,
-    ).astype(out_ref.dtype)
+def mix_kernel(comb_ref, ret_ref, out_ref, out, out_sem):
+    images = comb_ref.shape[0]
+    ret = ret_ref[...].astype(BF16)
+    copies = []
+    for i in range(images):
+        v = lax.dot_general(
+            comb_ref[i], ret, (((0,), (0,)), ((), ())), preferred_element_type=F32
+        )
+        out[i] = v.astype(out.dtype)
+        copies.append(pltpu.make_async_copy(out.at[i], out_ref.at[i], out_sem.at[i]))
+        copies[-1].start()
+    for copy in copies:
+        copy.wait()
 
 
 def body(tokens, slot_keys, logit_scale, up_weight, up_bias, down_weight, down_bias):
@@ -337,20 +380,24 @@
     comb, ret = pl.pallas_call(
         functools.partial(route_and_experts, owners, n_dp, chunk),
         out_shape=(
-            jax.ShapeDtypeStruct((images, slots, patches), BF16),
-            jax.ShapeDtypeStruct((slots, width), F32),
+            pltpu.VMEM((images, slots, patches), BF16),
+            pltpu.VMEM((slots, width), F32),
         ),
         in_specs=[
             hbm,
-            vmem,
-            pl.BlockSpec(memory_space=pltpu.SMEM),
-            hbm,
-            vmem,
-            hbm,
-            vmem,
+            hbm,
+            pl.BlockSpec(memory_space=pltpu.HBM),
+            hbm,
+            hbm,
+            hbm,
+            hbm,
         ],
         out_specs=(vmem, vmem),
         scratch_shapes=[
+            pltpu.VMEM((owners, width), BF16),
+            pltpu.SMEM((1,), F32),
+            pltpu.VMEM(up_bias.shape, BF16),
+            pltpu.VMEM(down_bias.shape, BF16),
             pltpu.VMEM((images, patches, width), BF16),
             pltpu.VMEM((width, hidden), BF16),
             pltpu.VMEM((hidden, width), BF16),
@@ -363,6 +410,7 @@
             pltpu.VMEM((pieces, rows, chunk), BF16),
             pltpu.VMEM((groups, images, width), BF16),
             pltpu.VMEM((groups, images, width), BF16),
+            dma((4,)),
             dma((images,)),
             dma((2,)),
             dma((2,)),
@@ -379,18 +427,18 @@
             collective_id=0, has_side_effects=True, vmem_limit_bytes=60 * 1024 * 1024
         ),
         name="route_and_experts",
-    )(tokens, slot_keys, logit_scale, up_weight, up_bias, down_weight, down_bias)
+    )(tokens, slot_keys.T, logit_scale, up_weight, up_bias, down_weight, down_bias)
     return pl.pallas_call(
         mix_kernel,
-        grid=(images,),
         out_shape=jax.ShapeDtypeStruct(tokens.shape, BF16),
-        in_specs=[
-            pl.BlockSpec((1, slots, patches), lambda i: (i, 0, 0)),
-            pl.BlockSpec((slots, width), lambda i: (0, 0)),
-        ],
-        out_specs=pl.BlockSpec((1, patches, width), lambda i: (i, 0, 0)),
+        in_specs=[vmem, vmem],
+        out_specs=hbm,
+        scratch_shapes=[pltpu.VMEM(tokens.shape, BF16), dma((images,))],
         name="mix_tokens",
-    )(comb, ret)
+    )(
+        pltpu.with_memory_space_constraint(comb, pltpu.VMEM),
+        pltpu.with_memory_space_constraint(ret, pltpu.VMEM),
+    )
 
 
 def solution(mesh):

time: 32.3 us -> 27 us (0.84)
  Pallas kernels: 29.7 us -> 26.2 us
  local copies, waits for them, and re-layouts: 1.62 us -> 0 us
    pallas_call x1, Pallas kernels: 4.04 us -> 1.9 us  [body(): pl.pallas_call(mix_kernel, out_shape=jax.ShapeDtypeStruct(tokens.shape, B...]
    unnamed x1 -> x0, local copies, waits for them, and re-layouts: 1.62 us -> none
    pallas_call x1, Pallas kernels: 25.7 us -> 24.3 us  [body(): pl.pallas_call(functools.partial(route_and_experts, owners, n_dp, chunk),...]
where the time goes in v2:
time: 27 us; the launch traced here: 26.9 us
  Pallas kernels  26.2 us (97%)
  between operations  0.66 us (2%)
    pallas_call x1, Pallas kernels, body(): pl.pallas_call(functools.partial(route_and_experts, owners, n_dp, chunk),...  24.3 us
    pallas_call x1, Pallas kernels, body(): pl.pallas_call(mix_kernel, out_shape=jax.ShapeDtypeStruct(tokens.shape, B...  1.9 us

profile of v2, /device:TPU:0, one launch (start us, length us, event | category | flops | bytes accessed | tf_op | source)
XLA Modules:
  0.0 26.9 jit_solution(10704816339094398419)
XLA Ops:
  0.7 24.3 %route_and_experts.1 = (bf16[4,32,256]{2,1,0:T(8,128)(2,1)S(1)}, f32[32,1280]{1,0:T(8,128)S(1)}) custom-call(bf16[4,256,1280]{2,1,0:T(8,128)(2,1)} %tok_hbm.1, bf16[8,1280]{1,0:T(8,128)(2,1)} %bitcast.1, f32[1]{0:T(128)S(6)} %copy.8.scale_hbm, bf16[1,1280,1280]{2,1,0:T(8,128)(2,1)} %w1_hbm.1, bf16[1,1280]{1,0:T(2,128)(2,1)} %b1_hbm.1, ...), custom_call_target="tpu_custom_call" | custom-call | tf_op jit(solution)/shard_map/route_and_experts/pallas_call | solution.py:380
  25.0 1.9 %mix_tokens.1 = bf16[4,256,1280]{2,1,0:T(8,128)(2,1)} custom-call(bf16[4,32,256]{2,1,0:T(8,128)(2,1)S(1)} %get-tuple-element.7.comb_ref, f32[32,1280]{1,0:T(8,128)S(1)} %get-tuple-element.8.ret_ref), custom_call_target="tpu_custom_call" | custom-call | tf_op jit(solution)/shard_map/mix_tokens/pallas_call | solution.py:431

commit v3 on v2

--- a/solution.py
+++ b/solution.py
@@ -244,7 +244,7 @@
 
     def pair_copy(j):
         return pltpu.make_async_remote_copy(
-            src_ref=part.at[j, other],
+            src_ref=part.at[j, pl.ds(pl.multiple_of(other * rows, rows), rows)],
             dst_ref=pair.at[j],
             send_sem=p_send.at[j],
             recv_sem=p_recv.at[j],
@@ -254,18 +254,16 @@
 
     pieces = width // chunk
     for j in range(pieces):
-        for side in range(CORES):
-
-            def second(m, c):
-                at = pl.multiple_of(m * block2, block2)
-                h = hid[pl.ds(side * rows + at, block2), :]
-                v = jnp.dot(h, w2[:, j * chunk : (j + 1) * chunk], preferred_element_type=F32)
-                part[j, side, pl.ds(at, block2), :] = v.astype(BF16)
-                mine[j, side, pl.ds(at, block2), :] = v
-                return c
-
-            block2 = min(128, rows)
-            lax.fori_loop(0, rows // block2, second, 0, unroll=rows == block2)
+
+        def second(m, c):
+            at = pl.multiple_of(m * block, block)
+            h = hid[pl.ds(at, block), :]
+            v = jnp.dot(h, w2[:, j * chunk : (j + 1) * chunk], preferred_element_type=F32)
+            part[j, pl.ds(at, block), :] = v.astype(BF16)
+            mine[j, pl.ds(at, block), :] = v
+            return c
+
+        lax.fori_loop(0, steps, second, 0, unroll=steps == 1)
         pair_copy(j).start()
 
     for j in range(pieces):
@@ -273,7 +271,8 @@
 
         def join(k, c):
             at = pl.multiple_of(k * 4 * images, 4 * images)
-            v = mine[j, core, pl.ds(at, 4 * images), :]
+            own_at = pl.multiple_of(core * rows + at, 4 * images)
+            v = mine[j, pl.ds(own_at, 4 * images), :]
             v = v + pair[j, pl.ds(at, 4 * images), :].astype(F32)
             for q in range(4):
                 back[4 * k + q, :, j * chunk : (j + 1) * chunk] = v[
@@ -405,8 +404,8 @@
             pltpu.VMEM((CORES, groups, images, width), BF16),
             pltpu.VMEM((CORES * rows, width), F32),
             pltpu.VMEM((CORES * rows, hidden), BF16),
-            pltpu.VMEM((pieces, CORES, rows, chunk), BF16),
-            pltpu.VMEM((pieces, CORES, rows, chunk), F32),
+            pltpu.VMEM((pieces, CORES * rows, chunk), BF16),
+            pltpu.VMEM((pieces, CORES * rows, chunk), F32),
             pltpu.VMEM((pieces, rows, chunk), BF16),
             pltpu.VMEM((groups, images, width), BF16),
             pltpu.VMEM((groups, images, width), BF16),

time: 27 us -> 26.9 us (level)
  no operation moved by 1% of the time
where the time goes in v3:
time: 26.9 us; the launch traced here: 26.7 us
  Pallas kernels  26 us (97%)
  between operations  0.66 us (2%)
    pallas_call x1, Pallas kernels, body(): pl.pallas_call(functools.partial(route_and_experts, owners, n_dp, chunk),...  24.1 us
    pallas_call x1, Pallas kernels, body(): pl.pallas_call(mix_kernel, out_shape=jax.ShapeDtypeStruct(tokens.shape, B...  1.9 us

profile of v3, /device:TPU:0, one launch (start us, length us, event | category | flops | bytes accessed | tf_op | source)
XLA Modules:
  0.0 26.7 jit_solution(14630952298551950206)
XLA Ops:
  0.7 24.1 %route_and_experts.1 = (bf16[4,32,256]{2,1,0:T(8,128)(2,1)S(1)}, f32[32,1280]{1,0:T(8,128)S(1)}) custom-call(bf16[4,256,1280]{2,1,0:T(8,128)(2,1)} %tok_hbm.1, bf16[8,1280]{1,0:T(8,128)(2,1)} %bitcast.1, f32[1]{0:T(128)S(6)} %copy.8.scale_hbm, bf16[1,1280,1280]{2,1,0:T(8,128)(2,1)} %w1_hbm.1, bf16[1,1280]{1,0:T(2,128)(2,1)} %b1_hbm.1, ...), custom_call_target="tpu_custom_call" | custom-call | tf_op jit(solution)/shard_map/route_and_experts/pallas_call | solution.py:379
  24.8 1.9 %mix_tokens.1 = bf16[4,256,1280]{2,1,0:T(8,128)(2,1)} custom-call(bf16[4,32,256]{2,1,0:T(8,128)(2,1)S(1)} %get-tuple-element.7.comb_ref, f32[32,1280]{1,0:T(8,128)S(1)} %get-tuple-element.8.ret_ref), custom_call_target="tpu_custom_call" | custom-call | tf_op jit(solution)/shard_map/mix_tokens/pallas_call | solution.py:430
